TPU v7x, 32 devices: a whole 2x2x4 slice. The times are simulated.
32 devices in a mesh: lon: 8 (over y, x, core), lat: 4 (over z).
Axes of the slice: x: 2, y: 2, z: 4, core: 2. Of those that a mesh axis runs over, the one named last changes fastest.
Arguments:
- fields: bfloat16 [32, 256, 256], P('lat', 'lon'), may hold values from -6 to 6
- norm_lon: float32 [256], replicated, may hold values from 0.25 to 1.75
- query_lon: bfloat16 [256, 256], replicated, may hold values from -0.375 to 0.375
- key_lon: bfloat16 [256, 256], replicated, may hold values from -0.375 to 0.375
- value_lon: bfloat16 [256, 256], replicated, may hold values from -0.375 to 0.375
- out_lon: bfloat16 [256, 256], replicated, may hold values from -0.375 to 0.375
- temp_lon: float32 [8], replicated, may hold values from 0.5 to 12
- bias_lon: float32 [8], replicated, may hold values from -2 to 2
- norm_lat: float32 [256], replicated, may hold values from 0.25 to 1.75
- query_lat: bfloat16 [256, 256], replicated, may hold values from -0.375 to 0.375
- key_lat: bfloat16 [256, 256], replicated, may hold values from -0.375 to 0.375
- value_lat: bfloat16 [256, 256], replicated, may hold values from -0.375 to 0.375
- out_lat: bfloat16 [256, 256], replicated, may hold values from -0.375 to 0.375
- temp_lat: float32 [8], replicated, may hold values from 0.5 to 12
- bias_lat: float32 [8], replicated, may hold values from -4 to 0
- norm_mlp: float32 [256], replicated, may hold values from 0.25 to 1.75
- w_gate: bfloat16 [256, 1024], replicated, may hold values from -0.375 to 0.375
- w_up: bfloat16 [256, 1024], replicated, may hold values from -0.375 to 0.375
- w_down: bfloat16 [1024, 256], replicated, may hold values from -0.1875 to 0.1875
Outputs:
- updated: bfloat16 [32, 256, 256], P('lat', 'lon')
All inputs are finite; a program needn't handle non-finite values.
Results may differ from a plain program's by a relative error of at most 0.018.
The roundings to bfloat16 on the way count: a program that leaves them out, or rounds other values in their place, can miss the bound.
Values may be sent and summed in bfloat16 or wider, within the bound.
A program may use at most 64 MiB of HBM per device.

v0:
```python
import math

import jax
import jax.numpy as jnp
from jax import lax
from jax.sharding import PartitionSpec as P


def normalize(values, gain):
    factor = lax.rsqrt(jnp.mean(values * values, axis=-1, keepdims=True) + 1e-06)
    return (values * factor * gain).astype(jnp.bfloat16)


def project(values, weight):
    return jnp.dot(values, weight, preferred_element_type=jnp.float32).astype(jnp.bfloat16)


def attend_lat(queries, keys, values, temp, bias):
    count, cols, depth = queries.shape
    heads = temp.shape[0]
    size = depth // heads
    qh = queries.reshape(count, cols, heads, size)
    kh = keys.reshape(count, cols, heads, size)
    vh = values.reshape(count, cols, heads, size)
    scores = jnp.einsum("ichd,jchd->chij", qh, kh, preferred_element_type=jnp.float32)
    place = jnp.arange(count, dtype=jnp.int32)
    spread = jnp.abs(place[:, None] - place[None, :]).astype(jnp.float32) / count
    scores = (
        scores * (temp / math.sqrt(size))[None, :, None, None]
        + bias[None, :, None, None] * spread[None, None]
    )
    expo = jnp.exp(scores - jnp.max(scores, axis=-1, keepdims=True))
    denom = jnp.sum(expo, axis=-1)
    mixed = jnp.einsum(
        "chij,jchd->ichd", expo.astype(jnp.bfloat16), vh, preferred_element_type=jnp.float32
    )
    mixed = mixed / jnp.transpose(denom, (2, 0, 1))[..., None]
    return mixed.astype(jnp.bfloat16).reshape(count, cols, depth)


def body(
    fields,
    norm_lon,
    query_lon,
    key_lon,
    value_lon,
    out_lon,
    temp_lon,
    bias_lon,
    norm_lat,
    query_lat,
    key_lat,
    value_lat,
    out_lat,
    temp_lat,
    bias_lat,
    norm_mlp,
    w_gate,
    w_up,
    w_down,
):
    rows, width, depth = fields.shape
    heads = temp_lon.shape[0]
    size = depth // heads
    total_lon = width * lax.axis_size("lon")
    resid = fields.astype(jnp.float32)
    normed = normalize(resid, norm_lon)
    scale_lon = temp_lon / math.sqrt(size)
    query_place = lax.axis_index("lon") * width + jnp.arange(width, dtype=jnp.int32)
    queries = project(normed, query_lon).reshape(rows, width, heads, size)
    piece = lax.all_gather(normed, "lon", axis=1, tiled=True)
    keys = project(piece, key_lon)
    count = keys.shape[1]
    key_place = jnp.arange(count, dtype=jnp.int32)
    angle = (query_place[:, None] - key_place[None, :]).astype(jnp.float32) * (
        2.0 * math.pi / total_lon
    )
    wave = jnp.cos(angle)

    def one_row(items):
        query_row, key_row, value_row, peak, total, accum = items
        key_heads = key_row.reshape(count, heads, size)
        value_heads = value_row.reshape(count, heads, size)
        scores = jnp.einsum(
            "ihd,jhd->hij", query_row, key_heads, preferred_element_type=jnp.float32
        )
        scores = scores * scale_lon[:, None, None] + bias_lon[:, None, None] * wave[None]
        fresh = jnp.maximum(peak, jnp.max(scores, axis=-1))
        shrink = jnp.exp(peak - fresh)
        expo = jnp.exp(scores - fresh[..., None])
        total = total * shrink + jnp.sum(expo, axis=-1)
        mixed = jnp.einsum(
            "hij,jhd->ihd",
            expo.astype(jnp.bfloat16),
            value_heads,
            preferred_element_type=jnp.float32,
        )
        accum = accum.reshape(width, heads, size) * jnp.transpose(shrink)[:, :, None] + mixed
        return (fresh, total, accum.reshape(width, depth))

    peak = jnp.full((rows, heads, width), -1e30, jnp.float32)
    total = jnp.zeros((rows, heads, width), jnp.float32)
    accum = jnp.zeros((rows, width, depth), jnp.float32)
    peak, total, accum = lax.map(
        one_row, (queries, keys, project(piece, value_lon), peak, total, accum)
    )
    attended = accum.reshape(rows, width, heads, size) / jnp.transpose(total, (0, 2, 1))[..., None]
    attended = attended.astype(jnp.bfloat16).reshape(rows, width, depth)
    first = resid + jnp.dot(attended, out_lon, preferred_element_type=jnp.float32)
    normed_lat = normalize(first, norm_lat)
    query_col = project(normed_lat, query_lat)
    key_col = project(normed_lat, key_lat)
    value_col = project(normed_lat, value_lat)
    query_col, key_col, value_col = (
        lax.all_to_all(query_col, "lat", split_axis=1, concat_axis=0, tiled=True),
        lax.all_to_all(key_col, "lat", split_axis=1, concat_axis=0, tiled=True),
        lax.all_to_all(value_col, "lat", split_axis=1, concat_axis=0, tiled=True),
    )
    mixed_lat = attend_lat(query_col, key_col, value_col, temp_lat, bias_lat)
    returned = lax.all_to_all(mixed_lat, "lat", split_axis=0, concat_axis=1, tiled=True)
    second = first + jnp.dot(returned, out_lat, preferred_element_type=jnp.float32)
    normed_mlp = normalize(second, norm_mlp)
    gate = jnp.dot(normed_mlp, w_gate, preferred_element_type=jnp.float32)
    upper = jnp.dot(normed_mlp, w_up, preferred_element_type=jnp.float32)
    hidden = (jax.nn.silu(gate) * upper).astype(jnp.bfloat16)
    return (second + jnp.dot(hidden, w_down, preferred_element_type=jnp.float32)).astype(
        jnp.bfloat16
    )


def solution(mesh):
    in_specs = (
        P("lat", "lon", None),
        P(),
        P(),
        P(),
        P(),
        P(),
        P(),
        P(),
        P(),
        P(),
        P(),
        P(),
        P(),
        P(),
        P(),
        P(),
        P(),
        P(),
        P(),
    )
    out_specs = P("lat", "lon", None)
    return jax.shard_map(body, mesh=mesh, in_specs=in_specs, out_specs=out_specs, check_vma=False)
```

profile of v0, /device:TPU:0, one launch (start us, length us, event | category | flops | bytes accessed | tf_op | source)
XLA Modules:
  0.0 112.4 jit_solution(1554158160764497591)
XLA Ops:
  6.6 1.1 fusion.35
  7.7 1.7 %fusion.37 = bf16[8,32,256]{2,1,0:T(8,128)(2,1)} fusion(bf16[8,32,256]{2,1,0:T(8,128)(2,1)} %param.21, f32[256]{0:T(256)} %param.22, f32[8,32]{1,0:T(8,128)S(1)} %add_rsqrt_fusion.2), kind=kLoop, calls=%fused_computation.60 | loop fusion | flops 262144 | bytes 264192 | tf_op jit(solution)/shard_map/convert_element_type | solution.py:11
  9.4 1.2 %convolution_convert_fusion.5 = bf16[8,32,256]{2,1,0:T(8,128)(2,1)S(1)} fusion(bf16[8,32,256]{2,1,0:T(8,128)(2,1)} %fusion.37, bf16[256,256]{1,0:T(8,128)(2,1)} %param.23), kind=kOutput, calls=%fused_computation.36 | convolution fusion | flops 33619968 | bytes 393216 | tf_op jit(solution)/shard_map/dot_general | solution.py:15
  10.6 1.0 reshape.126
  11.7 23.9 %all-gather.2.cloned.1.call-done = bf16[8,256,256]{2,1,0:T(8,128)(2,1)} async-done(((bf16[8,32,256]{2,1,0:T(8,128)(2,1)}), bf16[8,256,256]{2,1,0:T(8,128)(2,1)}) %all-gather.2.cloned.1.call-update) | async-done | bytes 1048592 | tf_op jit(solution)/shard_map/all_gather | solution.py:71
  35.6 1.7 %convolution_convert_fusion.1 = bf16[8,256,256]{2,1,0:T(8,128)(2,1)S(1)} fusion(bf16[8,256,256]{2,1,0:T(8,128)(2,1)} %all-gather.2.cloned.1.call-done, bf16[256,256]{1,0:T(8,128)(2,1)S(1)} %copy-done.3), kind=kOutput, calls=%fused_computation.20 | convolution fusion | flops 268959744 | bytes 2228224 | tf_op jit(solution)/shard_map/dot_general | solution.py:15
  38.1 21.5 %while.13 = (s32[]{:T(128)}, f32[8,8,32]{2,1,0:T(8,128)S(1)}, f32[8,32,256]{1,2,0:T(8,128)}, bf16[8,32,8,32]{3,2,1,0:T(8,128)(2,1)}, bf16[8,256,256]{2,1,0:T(8,1...) while((s32[]{:T(128)}, f32[8,8,32]{2,1,0:T(8,128)S(1)}, ...), condition=%wide.region_4.5_spmd.clone, body=%wide.region_1.4_spmd.clone.sunk | while | flops 8946946 | bytes 2429245 | solution.py:104
  38.4 0.9 constant_dynamic-slice_fusion.6
  40.1 0.7 constant_dynamic-update-slice_fusion.2
  41.1 0.9 constant_dynamic-slice_fusion.6
  43.8 0.9 constant_dynamic-slice_fusion.6
  45.5 0.7 constant_dynamic-update-slice_fusion.2
  46.5 0.9 constant_dynamic-slice_fusion.6
  49.1 0.9 constant_dynamic-slice_fusion.6
  51.8 0.9 constant_dynamic-slice_fusion.6
  53.5 0.7 constant_dynamic-update-slice_fusion.2
  54.5 0.9 constant_dynamic-slice_fusion.6
  56.2 0.7 constant_dynamic-update-slice_fusion.2
  57.2 0.9 constant_dynamic-slice_fusion.6
  59.5 1.4 %fusion.16 = bf16[8,32,256]{1,2,0:T(8,128)(2,1)S(1)} fusion(f32[8,32,256]{1,2,0:T(8,128)} %get-tuple-element.53, f32[8,32,8]{1,2,0:T(8,128)S(1)} %bitcast.131), kind=kLoop, calls=%fused_computation.38 | loop fusion | flops 131072 | bytes 401408 | tf_op jit(solution)/shard_map/convert_element_type | solution.py:108
  62.0 0.7 copy.48
  62.8 4.7 %all-to-all-start.2 = ((bf16[8,32,256]{2,0,1:T(8,128)(2,1)}), bf16[8,32,256]{2,0,1:T(8,128)(2,1)S(1)}, u32[]{:S(2)}, u32[]{:S(2)}) async-start(bf16[8,32,256]{2,0,1:T(8,128)(2,1)} %copy.48), calls=%async_computation.2 | async-start | bytes 262144 | tf_op jit(solution)/shard_map/all_to_all | solution.py:116
  67.7 0.7 copy.46
  68.4 5.4 %all-to-all-done.2 = bf16[8,32,256]{2,0,1:T(8,128)(2,1)S(1)} async-done(((bf16[8,32,256]{2,0,1:T(8,128)(2,1)}), bf16[8,32,256]{2,0,1:T(8,128)(2,1)S(1)}, u32[]{:S(2)}, u32[]{:S(2)}) %all-to-all-start.2) | async-done | bytes 131104 | tf_op jit(solution)/shard_map/all_to_all | solution.py:116
  73.8 3.3 %all-to-all-start.1 = ((bf16[8,32,256]{2,0,1:T(8,128)(2,1)}), bf16[8,32,256]{2,0,1:T(8,128)(2,1)S(1)}, u32[]{:S(2)}, u32[]{:S(2)}) async-start(bf16[8,32,256]{2,0,1:T(8,128)(2,1)} %copy.46), calls=%async_computation.1 | async-start | bytes 262144 | tf_op jit(solution)/shard_map/all_to_all | solution.py:115
  77.3 0.7 copy.44
  78.0 5.0 %all-to-all-done.1 = bf16[8,32,256]{2,0,1:T(8,128)(2,1)S(1)} async-done(((bf16[8,32,256]{2,0,1:T(8,128)(2,1)}), bf16[8,32,256]{2,0,1:T(8,128)(2,1)S(1)}, u32[]{:S(2)}, u32[]{:S(2)}) %all-to-all-start.1) | async-done | bytes 131104 | tf_op jit(solution)/shard_map/all_to_all | solution.py:115
  83.0 3.3 %all-to-all-start = ((bf16[8,32,256]{2,0,1:T(8,128)(2,1)}), bf16[8,32,256]{2,0,1:T(8,128)(2,1)S(1)}, u32[]{:S(2)}, u32[]{:S(2)}) async-start(bf16[8,32,256]{2,0,1:T(8,128)(2,1)} %copy.44), calls=%async_computation | async-start | bytes 262144 | tf_op jit(solution)/shard_map/all_to_all | solution.py:117
  86.9 5.3 %all-to-all-done = bf16[8,32,256]{2,0,1:T(8,128)(2,1)S(1)} async-done(((bf16[8,32,256]{2,0,1:T(8,128)(2,1)}), bf16[8,32,256]{2,0,1:T(8,128)(2,1)S(1)}, u32[]{:S(2)}, u32[]{:S(2)}) %all-to-all-start) | async-done | bytes 131104 | tf_op jit(solution)/shard_map/all_to_all | solution.py:117
  92.5 0.9 fusion.56
  94.5 8.4 %all_to_all.63 = bf16[32,8,256]{2,1,0:T(8,128)(2,1)S(1)} all-to-all(bf16[32,8,256]{2,1,0:T(8,128)(2,1)S(1)} %copy.54), channel_id=1, replica_groups=mesh['lon'=8,'lat'=4] {'lat'}, dimensions={0} | all-to-all | bytes 262144 | tf_op jit(solution)/shard_map/all_to_all | solution.py:120
  104.4 1.2 %fusion.15 = bf16[8,32,256]{2,1,0:T(8,128)(2,1)} fusion(f32[8,32,256]{2,1,0:T(8,128)S(1)} %get-tuple-element.132, f32[8,32,1024]{2,1,0:T(8,128)S(1)} %fusion.28, bf16[1024,256]{1,0:T(8,128)(2,1)S(1)} %copy-done.14, bf16[256,1024]{1,0:T(8,128)(2,1)S(1)} %copy-done.15, f32[256]{0:T(256)S(1)} %copy-done.12, f32[8,32]{1,0:T(8,128)S(1)} %add_rsqrt_fusion), kind=kOutput, calls=%fused_computation.32 | convolution fusion | flops 270336000 | bytes 2492416 | tf_op jit(solution)/shard_map/dot_general | solution.py:126
  (141 shorter events, 17.0 us)
Async XLA Ops:
  6.5 96.7 %copy-start = (bf16[256,1024]{1,0:T(8,128)(2,1)S(1)}, bf16[256,1024]{1,0:T(8,128)(2,1)}, u32[]{:S(2)}) copy-start(bf16[256,1024]{1,0:T(8,128)(2,1)} %param.37) | copy-start | bytes 1572868
  6.5 5.1 %copy-start.16 = (f32[8]{0:T(128)S(1)}, f32[8]{0:T(128)}, u32[]{:S(2)}) copy-start(f32[8]{0:T(128)} %param.27) | copy-start | bytes 100
  6.5 5.1 %copy-start.13 = (f32[8]{0:T(128)S(1)}, f32[8]{0:T(128)}, u32[]{:S(2)}) copy-start(f32[8]{0:T(128)} %param.35) | copy-start | bytes 100
  6.5 29.1 %copy-start.3 = (bf16[256,256]{1,0:T(8,128)(2,1)S(1)}, bf16[256,256]{1,0:T(8,128)(2,1)}, u32[]{:S(2)}) copy-start(bf16[256,256]{1,0:T(8,128)(2,1)} %param.24) | copy-start | bytes 393220
  6.5 29.1 %all-gather.2.cloned.1.call-start = ((), (), s32[]{:S(2)}) async-start(), calls=%async_computation.4 | async-start | bytes 1179648 | tf_op jit(solution)/shard_map/all_gather | solution.py:71
  11.7 25.7 %copy-start.4 = (bf16[256,256]{1,0:T(8,128)(2,1)S(1)}, bf16[256,256]{1,0:T(8,128)(2,1)}, u32[]{:S(2)}) copy-start(bf16[256,256]{1,0:T(8,128)(2,1)} %param.25) | copy-start | bytes 393220
  35.6 1.8 %copy-start.1 = (bf16[8,256,256]{2,1,0:T(8,128)(2,1)S(1)}, bf16[8,256,256]{2,1,0:T(8,128)(2,1)}, u32[]{:S(2)}) copy-start(bf16[8,256,256]{2,1,0:T(8,128)(2,1)} %all-gather.2.cloned.1.call-done) | copy-start | bytes 3145732
  37.4 0.7 copy-start.10
  59.5 1.4 %copy-start.2 = (bf16[8,32,256]{2,1,0:T(8,128)(2,1)S(1)}, bf16[8,32,256]{2,1,0:T(8,128)(2,1)}, u32[]{:S(2)}) copy-start(bf16[8,32,256]{2,1,0:T(8,128)(2,1)} %param.21) | copy-start | bytes 393220
  59.5 1.4 %copy-start.9 = (bf16[256,256]{1,0:T(8,128)(2,1)S(1)}, bf16[256,256]{1,0:T(8,128)(2,1)}, u32[]{:S(2)}) copy-start(bf16[256,256]{1,0:T(8,128)(2,1)} %param.26) | copy-start | bytes 393220
  59.5 1.8 %copy-start.11 = (f32[256]{0:T(256)S(1)}, f32[256]{0:T(256)}, u32[]{:S(2)}) copy-start(f32[256]{0:T(256)} %param.29) | copy-start | bytes 3076
  60.9 0.9 copy-start.5
  60.9 6.5 %copy-start.6 = (bf16[256,256]{1,0:T(8,128)(2,1)S(1)}, bf16[256,256]{1,0:T(8,128)(2,1)}, u32[]{:S(2)}) copy-start(bf16[256,256]{1,0:T(8,128)(2,1)} %param.30) | copy-start | bytes 393220
  61.4 15.7 %copy-start.7 = (bf16[256,256]{1,0:T(8,128)(2,1)S(1)}, bf16[256,256]{1,0:T(8,128)(2,1)}, u32[]{:S(2)}) copy-start(bf16[256,256]{1,0:T(8,128)(2,1)} %param.32) | copy-start | bytes 393220
  62.8 23.6 %copy-start.17 = (f32[8]{0:T(128)S(1)}, f32[8]{0:T(128)}, u32[]{:S(2)}) copy-start(f32[8]{0:T(128)} %param.34) | copy-start | bytes 100
  62.8 11.0 %all-to-all-start.2 = ((bf16[8,32,256]{2,0,1:T(8,128)(2,1)}), bf16[8,32,256]{2,0,1:T(8,128)(2,1)S(1)}, u32[]{:S(2)}, u32[]{:S(2)}) async-start(bf16[8,32,256]{2,0,1:T(8,128)(2,1)} %copy.48), calls=%async_computation.2 | async-start | bytes 262144 | tf_op jit(solution)/shard_map/all_to_all | solution.py:116
  73.8 9.2 %all-to-all-start.1 = ((bf16[8,32,256]{2,0,1:T(8,128)(2,1)}), bf16[8,32,256]{2,0,1:T(8,128)(2,1)S(1)}, u32[]{:S(2)}, u32[]{:S(2)}) async-start(bf16[8,32,256]{2,0,1:T(8,128)(2,1)} %copy.46), calls=%async_computation.1 | async-start | bytes 262144 | tf_op jit(solution)/shard_map/all_to_all | solution.py:115
  83.0 9.2 %all-to-all-start = ((bf16[8,32,256]{2,0,1:T(8,128)(2,1)}), bf16[8,32,256]{2,0,1:T(8,128)(2,1)S(1)}, u32[]{:S(2)}, u32[]{:S(2)}) async-start(bf16[8,32,256]{2,0,1:T(8,128)(2,1)} %copy.44), calls=%async_computation | async-start | bytes 262144 | tf_op jit(solution)/shard_map/all_to_all | solution.py:117
  93.6 9.2 %copy-start.8 = (bf16[256,256]{1,0:T(8,128)(2,1)S(1)}, bf16[256,256]{1,0:T(8,128)(2,1)}, u32[]{:S(2)}) copy-start(bf16[256,256]{1,0:T(8,128)(2,1)} %param.33) | copy-start | bytes 393220
  94.2 9.0 %copy-start.12 = (f32[256]{0:T(256)S(1)}, f32[256]{0:T(256)}, u32[]{:S(2)}) copy-start(f32[256]{0:T(256)} %param.36) | copy-start | bytes 3076
  103.1 1.0 copy-start.14
  103.2 1.2 %copy-start.15 = (bf16[256,1024]{1,0:T(8,128)(2,1)S(1)}, bf16[256,1024]{1,0:T(8,128)(2,1)}, u32[]{:S(2)}) copy-start(bf16[256,1024]{1,0:T(8,128)(2,1)} %param.38) | copy-start | bytes 1572868
Sparse Core Ops, SparseCore 0:
  9.5 26.0 all-gather.1
where the time goes:
time: 113 us; the launch traced here: 112 us
  waiting for transfers between devices  39.5 us (35%)
  local copies, waits for them, and re-layouts  19.6 us (17%)
  between operations  13.8 us (12%)
  starting transfers between devices  11.4 us (10%)
  matrix products  11.4 us (10%)
  blocking collectives  8.41 us (7%)
  other arithmetic  7.81 us (7%)
    all_gather x1, waiting for transfers between devices, body(): piece = lax.all_gather(normed, 'lon', axis=1, tiled=True)  23.9 us
    dynamic_slice x32, local copies, waits for them, and re-layouts, body(): lax.map(one_row, (queries, keys, project(piece, value_lon), peak, total,...  8.61 us
    all_to_all x1, blocking collectives, body(): lax.all_to_all(mixed_lat, 'lat', split_axis=0, concat_axis=1, tiled=True)  8.41 us
    all_to_all x1, waiting for transfers between devices, body(): lax.all_to_all(key_col, 'lat', split_axis=1, concat_axis=0, tiled=True)  5.37 us
    all_to_all x1, waiting for transfers between devices, body(): lax.all_to_all(value_col, 'lat', split_axis=1, concat_axis=0, tiled=True)  5.31 us
    dynamic_update_slice x8, local copies, waits for them, and re-layouts, body(): lax.map(one_row, (queries, keys, project(piece, value_lon), peak, total,...  5.3 us
    all_to_all x1, waiting for transfers between devices, body(): lax.all_to_all(query_col, 'lat', split_axis=1, concat_axis=0, tiled=True)  4.95 us
    all_to_all x1, starting transfers between devices, body(): lax.all_to_all(key_col, 'lat', split_axis=1, concat_axis=0, tiled=True)  4.72 us
  transfers between devices with their start and end apart: 4, of which 4 were waited for; matrix products, arithmetic and copies ran while one was open for 4% of the time, Pallas kernels for 0%

commit v1 on v0

--- a/solution.py
+++ b/solution.py
@@ -2,7 +2,11 @@
 
 import jax
 import jax.numpy as jnp
+import functools
+import numpy as np
 from jax import lax
+from jax.experimental import pallas as pl
+from jax.experimental.pallas import tpu as pltpu
 from jax.sharding import PartitionSpec as P
 
 
@@ -128,27 +132,265 @@
     )
 
 
+NT = (((1,), (1,)), ((), ()))
+MESH = pl.DeviceIdType.MESH
+F32 = jnp.float32
+BF16 = jnp.bfloat16
+
+
+def mm(a, b):
+    return jnp.dot(a, b, preferred_element_type=F32)
+
+
+def mm_nt(a, b):
+    return lax.dot_general(a, b, NT, preferred_element_type=F32)
+
+
+def iota(shape, dim):
+    return lax.broadcasted_iota(jnp.int32, shape, dim)
+
+
+def heads_t(keys, queries_t, values_t, temp, bias, table, mask, heads, size):
+    outs = []
+    for h in range(heads):
+        part = slice(h * size, (h + 1) * size)
+        scores = mm(keys[:, part], queries_t[part, :])
+        scores = scores * (temp[h] / math.sqrt(size)) + bias[h] * table
+        if mask is not None:
+            scores = scores + mask
+        expo = jnp.exp(scores - jnp.max(scores, axis=0, keepdims=True))
+        denom = jnp.sum(expo, axis=0, keepdims=True)
+        outs.append(mm(values_t[part, :], expo.astype(BF16)) / denom)
+    return jnp.concatenate(outs, axis=0).astype(BF16)
+
+
+def block_kernel(
+    n_lon, n_lat, rows, width, depth, heads,
+    fields, gain_lon, gain_lat, gain_mlp, temp_lon, bias_lon, temp_lat, bias_lat,
+    wave_h, wq1_h, wk1_h, wv1_h, wo1_h, wq2_h, wk2_h, wv2_h, wo2_h, wg_h, wu_h, wd_h,
+    out,
+    wave, wq1, wk1, wv1, wo1, wq2, wk2, wv2, wo2, wg, wu, wd,
+    norm_out, norm_in, field_out, field_in, att_out, att_in, upd_out,
+    local_sem, s1, r1, s2, r2, s3, r3, s4, r4,
+):
+    me_lon = lax.axis_index("lon")
+    me_lat = lax.axis_index("lat")
+    total = n_lon * n_lat
+    me = me_lon * n_lat + me_lat
+    size = depth // heads
+    cols = width // n_lat
+    count = n_lat * rows
+    cells = rows * width
+
+    loads = [
+        pltpu.make_async_copy(src, dst, local_sem.at[i])
+        for i, (src, dst) in enumerate(
+            [(wq1_h, wq1), (wk1_h, wk1), (wv1_h, wv1), (wave_h, wave), (wo1_h, wo1), (wq2_h, wq2),
+             (wk2_h, wk2), (wv2_h, wv2), (wo2_h, wo2), (wg_h, wg), (wu_h, wu), (wd_h, wd)]
+        )
+    ]
+    for load in loads:
+        load.start()
+
+    barrier = pltpu.get_barrier_semaphore()
+
+    def greet(step, carry):
+        peer = lax.rem(me + step, total)
+        pl.semaphore_signal(
+            barrier, inc=1, device_id=(peer // n_lat, lax.rem(peer, n_lat)), device_id_type=MESH
+        )
+        return carry
+
+    lax.fori_loop(1, total, greet, 0)
+
+    wide = fields[...].astype(F32)
+    norm_out[...] = normalize(wide, gain_lon[...][None])
+    pieces = wide.reshape(rows, n_lat, cols, depth).astype(BF16)
+    for a in range(n_lat):
+        field_out[a] = pieces[:, a]
+
+    pl.semaphore_wait(barrier, total - 1)
+
+    def send_norm(step):
+        peer = lax.rem(me_lon + step, n_lon)
+        return pltpu.make_async_remote_copy(
+            src_ref=norm_out.at[peer], dst_ref=norm_in.at[me_lon], send_sem=s1.at[step],
+            recv_sem=r1.at[step], device_id=(peer, me_lat), device_id_type=MESH,
+        )
+
+    def lat_copy(step, src, dst, ssem, rsem):
+        peer = lax.rem(me_lat + step, n_lat)
+        return pltpu.make_async_remote_copy(
+            src_ref=src.at[peer], dst_ref=dst.at[me_lat], send_sem=ssem.at[step],
+            recv_sem=rsem.at[step], device_id=(me_lon, peer), device_id_type=MESH,
+        )
+
+    sends1 = [send_norm(step) for step in range(1, n_lon)]
+    for copy in sends1:
+        copy.start()
+    sends2 = [lat_copy(step, field_out, field_in, s2, r2) for step in range(1, n_lat)]
+    for copy in sends2:
+        copy.start()
+    norm_in[pl.ds(me_lon, 1)] = norm_out[pl.ds(me_lon, 1)]
+    field_in[pl.ds(me_lat, 1)] = field_out[pl.ds(me_lat, 1)]
+
+    shape = (cells, cells)
+    lanes = iota(shape, 1)
+    subs = iota(shape, 0)
+    to_cols = (lax.rem(subs, count) * cols + subs // count == lanes).astype(F32).astype(BF16)
+    from_cols = (lax.rem(lanes, count) * cols + lanes // count == subs).astype(F32).astype(BF16)
+    eye = (lanes == subs).astype(F32).astype(BF16)
+    half = cells // 2
+    hs, hl = iota((half, half), 0), iota((half, half), 1)
+    spread = jnp.abs(lax.rem(hs, count) - lax.rem(hl, count)).astype(F32) / count
+    mask = jnp.where(hs // count == hl // count, 0.0, -1e30).astype(F32)
+
+    for load in loads[:4]:
+        load.wait()
+    wq_t = wq1[...].T
+    wv_t = wv1[...].T
+
+    for copy in sends1:
+        copy.wait_recv()
+
+    nlon = n_lon * width
+    normed = norm_in[...].reshape(nlon, depth)
+    keys = mm(normed, wk1[...]).astype(BF16)
+    queries_t = mm_nt(wq_t, normed).astype(BF16)
+    values_t = mm_nt(wv_t, normed).astype(BF16)
+    att_t = heads_t(keys, queries_t, values_t, temp_lon, bias_lon, wave[...], None, heads, size)
+    att = mm_nt(eye, att_t)
+    att_out[...] = att.reshape(total, cols, depth).astype(BF16)
+
+    my_row = me_lat * rows + me_lon
+
+    def att_copy(step):
+        peer = lax.rem(me + step, total)
+        return pltpu.make_async_remote_copy(
+            src_ref=att_out.at[peer], dst_ref=att_in.at[my_row], send_sem=s3.at[step],
+            recv_sem=r3.at[step], device_id=(peer // n_lat, lax.rem(peer, n_lat)),
+            device_id_type=MESH,
+        )
+
+    def start_att(step, carry):
+        att_copy(step).start()
+        return carry
+
+    def wait_att(step, carry):
+        att_copy(step).wait_recv()
+        return carry
+
+    def wait_att_send(step, carry):
+        att_copy(step).wait_send()
+        return carry
+
+    lax.fori_loop(1, total, start_att, 0)
+    att_in[pl.ds(my_row, 1)] = att_out[pl.ds(me, 1)]
+
+    for load in loads[4:]:
+        load.wait()
+    wq2_t = wq2[...].T
+    wv2_t = wv2[...].T
+    for copy in sends2:
+        copy.wait_recv()
+    lax.fori_loop(1, total, wait_att, 0)
+
+    resid = field_in[...].astype(F32).reshape(cells, depth)
+    attended = att_in[...].astype(F32).reshape(cells, depth).astype(BF16)
+    first = resid + mm(attended, wo1[...])
+    normed = mm(to_cols, normalize(first, gain_lat[...])).astype(BF16)
+    keys = mm(normed, wk2[...]).astype(BF16)
+    queries_t = mm_nt(wq2_t, normed).astype(BF16)
+    values_t = mm_nt(wv2_t, normed).astype(BF16)
+    parts = []
+    for part in (slice(0, half), slice(half, cells)):
+        parts.append(
+            heads_t(keys[part], queries_t[:, part], values_t[:, part], temp_lat, bias_lat,
+                    spread, mask, heads, size)
+        )
+    att_t = jnp.concatenate(parts, axis=1)
+    attended = mm_nt(from_cols, att_t).astype(BF16)
+    second = first + mm(attended, wo2[...])
+    normed = normalize(second, gain_mlp[...])
+    ff = wg.shape[1]
+    step_ff = min(ff, 256)
+    for f in range(0, ff, step_ff):
+        gate = mm(normed, wg[:, f:f + step_ff])
+        upper = mm(normed, wu[:, f:f + step_ff])
+        hidden = (gate / (1.0 + jnp.exp(-gate)) * upper).astype(BF16)
+        second = second + mm(hidden, wd[f:f + step_ff, :])
+    upd_out[...] = second.reshape(n_lat, rows, cols, depth).astype(BF16)
+
+    sends4 = [lat_copy(step, upd_out, out, s4, r4) for step in range(1, n_lat)]
+    for copy in sends4:
+        copy.start()
+    out[pl.ds(me_lat, 1)] = upd_out[pl.ds(me_lat, 1)]
+    for copy in sends1:
+        copy.wait_send()
+    for copy in sends2:
+        copy.wait_send()
+    lax.fori_loop(1, total, wait_att_send, 0)
+    for copy in sends4:
+        copy.wait()
+
+
+def fused_body(
+    fields, norm_lon, query_lon, key_lon, value_lon, out_lon, temp_lon, bias_lon,
+    norm_lat, query_lat, key_lat, value_lat, out_lat, temp_lat, bias_lat,
+    norm_mlp, w_gate, w_up, w_down,
+):
+    rows, width, depth = fields.shape
+    heads = temp_lon.shape[0]
+    n_lon, n_lat = lax.axis_size("lon"), lax.axis_size("lat")
+    cols = width // n_lat
+    nlon = width * n_lon
+    total = n_lon * n_lat
+    place = np.arange(nlon)
+    wave = np.cos((place[:, None] - place[None, :]) * (2.0 * math.pi / nlon)).astype(np.float32)
+    vmem = pl.BlockSpec(memory_space=pltpu.VMEM)
+    smem = pl.BlockSpec(memory_space=pltpu.SMEM)
+    hbm = pl.BlockSpec(memory_space=pl.ANY)
+    weights = (query_lon, key_lon, value_lon, out_lon, query_lat, key_lat, value_lat, out_lat,
+               w_gate, w_up, w_down)
+    dma = pltpu.SemaphoreType.DMA
+    updated = pl.pallas_call(
+        functools.partial(block_kernel, n_lon, n_lat, rows, width, depth, heads),
+        out_shape=jax.ShapeDtypeStruct((n_lat, rows, cols, depth), BF16),
+        in_specs=[vmem] * 4 + [smem] * 4 + [hbm] * 12,
+        out_specs=vmem,
+        scratch_shapes=[pltpu.VMEM((nlon, nlon), F32)]
+        + [pltpu.VMEM(w.shape, w.dtype) for w in weights]
+        + [
+            pltpu.VMEM((rows, width, depth), BF16),
+            pltpu.VMEM((n_lon, width, depth), BF16),
+            pltpu.VMEM((n_lat, rows, cols, depth), BF16),
+            pltpu.VMEM((n_lat, rows, cols, depth), BF16),
+            pltpu.VMEM((total, cols, depth), BF16),
+            pltpu.VMEM((n_lat * rows, cols, depth), BF16),
+            pltpu.VMEM((n_lat, rows, cols, depth), BF16),
+            dma((12,)),
+            dma((n_lon,)), dma((n_lon,)),
+            dma((n_lat,)), dma((n_lat,)),
+            dma((total,)), dma((total,)),
+            dma((n_lat,)), dma((n_lat,)),
+        ],
+        compiler_params=pltpu.CompilerParams(collective_id=0, has_side_effects=True),
+    )(
+        fields, norm_lon[None], norm_lat[None], norm_mlp[None], temp_lon, bias_lon, temp_lat, bias_lat,
+        jnp.asarray(wave), *weights,
+    )
+    return jnp.transpose(updated, (1, 0, 2, 3)).reshape(rows, width, depth)
+
+
+def choose(*args):
+    rows, width, _ = args[0].shape
+    n_lon, n_lat = lax.axis_size("lon"), lax.axis_size("lat")
+    if rows == n_lon and width % n_lat == 0 and width // n_lat == 8:
+        return fused_body(*args)
+    return body(*args)
+
+
 def solution(mesh):
-    in_specs = (
-        P("lat", "lon", None),
-        P(),
-        P(),
-        P(),
-        P(),
-        P(),
-        P(),
-        P(),
-        P(),
-        P(),
-        P(),
-        P(),
-        P(),
-        P(),
-        P(),
-        P(),
-        P(),
-        P(),
-        P(),
-    )
+    in_specs = (P("lat", "lon", None),) + (P(),) * 18
     out_specs = P("lat", "lon", None)
-    return jax.shard_map(body, mesh=mesh, in_specs=in_specs, out_specs=out_specs, check_vma=False)
+    return jax.shard_map(choose, mesh=mesh, in_specs=in_specs, out_specs=out_specs, check_vma=False)

time: 113 us -> 31.8 us (0.28)
  waiting for transfers between devices: 39.5 us -> 0 us
  Pallas kernels: 0 us -> 30.1 us
  local copies, waits for them, and re-layouts: 19.6 us -> 1.57 us
  between operations: 13.8 us -> 0.01 us
  matrix products: 11.4 us -> 0 us
  starting transfers between devices: 11.4 us -> 0 us
  blocking collectives: 8.41 us -> 0 us
  other arithmetic: 7.81 us -> 0 us
    pallas_call x0 -> x1, Pallas kernels: none -> 30.1 us  [fused_body(): pl.pallas_call(functools.partial(block_kernel, n_lon, n_lat, rows, width,...]
    all_gather x1 -> x0, waiting for transfers between devices: 23.9 us -> none  [body(): piece = lax.all_gather(normed, 'lon', axis=1, tiled=True)]
    all_to_all x3 -> x0, waiting for transfers between devices: 15.6 us -> none  [the longest x1 5.37 us: body(): lax.all_to_all(key_col, 'lat', split_axis=1, concat_axis=0, tiled=True)]
    dot_general x28 -> x0, matrix products: 11.4 us -> none  [the longest x6 3.88 us: project(): jnp.dot(values, weight, preferred_element_type=jnp.float32)]
    all_to_all x3 -> x0, starting transfers between devices: 11.4 us -> none  [the longest x1 4.72 us: body(): lax.all_to_all(key_col, 'lat', split_axis=1, concat_axis=0, tiled=True)]
    dynamic_slice x32 -> x0, local copies, waits for them, and re-layouts: 8.61 us -> none  [body(): lax.map(one_row, (queries, keys, project(piece, value_lon), peak, total,...]
    all_to_all x1 -> x0, blocking collectives: 8.41 us -> none  [body(): lax.all_to_all(mixed_lat, 'lat', split_axis=0, concat_axis=1, tiled=True)]
    dynamic_update_slice x8 -> x0, local copies, waits for them, and re-layouts: 5.3 us -> none  [body(): lax.map(one_row, (queries, keys, project(piece, value_lon), peak, total,...]
  transfers between devices with their start and end apart: 4 -> 0, of which waited for: 4 -> 0; matrix products, arithmetic and copies ran while one was open for 4% -> 0% of each run, Pallas kernels for 0% -> 0%
where the time goes in v1:
time: 31.8 us; the launch traced here: 31.7 us
  Pallas kernels  30.1 us (95%)
  local copies, waits for them, and re-layouts  1.57 us (5%)
    pallas_call x1, Pallas kernels, fused_body(): pl.pallas_call(functools.partial(block_kernel, n_lon, n_lat, rows, width,...  30.1 us
    reshape x1, local copies, waits for them, and re-layouts, fused_body(): return jnp.transpose(updated, (1, 0, 2, 3)).reshape(rows, width, depth)  1.57 us

profile of v1, /device:TPU:0, one launch (start us, length us, event | category | flops | bytes accessed | tf_op | source)
XLA Modules:
  0.0 31.7 jit_solution(8175580403550112717)
XLA Ops:
  0.0 30.1 %shard_map.190 = bf16[4,8,8,256]{3,2,1,0:T(8,128)(2,1)} custom-call(bf16[8,32,256]{2,1,0:T(8,128)(2,1)} %fields.1, f32[1,256]{1,0:T(1,128)} %bitcast.8, f32[1,256]{1,0:T(1,128)} %bitcast.9, f32[1,256]{1,0:T(1,128)} %bitcast.10, f32[8]{0:T(128)} %temp_lon.1, f32[8]{0:T(128)} %bias_lon.1, f32[8]{0:T(128)} %temp_lat.1, f32[8]{0:T(128)} %bias_lat.1, ...), custom_call_target="tpu_custom_call" | custom-call | tf_op jit(solution)/shard_map/pallas_call | solution.py:356
  30.1 1.6 %copy_bitcast_fusion = bf16[8,32,256]{2,1,0:T(8,128)(2,1)} fusion(bf16[4,8,8,256]{3,2,1,0:T(8,128)(2,1)} %shard_map.190), kind=kLoop, calls=%fused_computation | loop fusion | bytes 262144 | tf_op jit(solution)/shard_map/reshape | solution.py:382

commit v2 on v1

--- a/solution.py
+++ b/solution.py
@@ -155,7 +155,7 @@
     for h in range(heads):
         part = slice(h * size, (h + 1) * size)
         scores = mm(keys[:, part], queries_t[part, :])
-        scores = scores * (temp[h] / math.sqrt(size)) + bias[h] * table
+        scores = scores * (temp[:, h:h + 1] / math.sqrt(size)) + bias[:, h:h + 1] * table
         if mask is not None:
             scores = scores + mask
         expo = jnp.exp(scores - jnp.max(scores, axis=0, keepdims=True))
@@ -166,9 +166,10 @@
 
 def block_kernel(
     n_lon, n_lat, rows, width, depth, heads,
-    fields, gain_lon, gain_lat, gain_mlp, temp_lon, bias_lon, temp_lat, bias_lat,
+    fields_h, gain_lon_h, gain_lat_h, gain_mlp_h, temp_lon_h, bias_lon_h, temp_lat_h, bias_lat_h,
     wave_h, wq1_h, wk1_h, wv1_h, wo1_h, wq2_h, wk2_h, wv2_h, wo2_h, wg_h, wu_h, wd_h,
     out,
+    fields, gain_lon, gain_lat, gain_mlp, temp_lon, bias_lon, temp_lat, bias_lat,
     wave, wq1, wk1, wv1, wo1, wq2, wk2, wv2, wo2, wg, wu, wd,
     norm_out, norm_in, field_out, field_in, att_out, att_in, upd_out,
     local_sem, s1, r1, s2, r2, s3, r3, s4, r4,
@@ -182,16 +183,6 @@
     count = n_lat * rows
     cells = rows * width
 
-    loads = [
-        pltpu.make_async_copy(src, dst, local_sem.at[i])
-        for i, (src, dst) in enumerate(
-            [(wq1_h, wq1), (wk1_h, wk1), (wv1_h, wv1), (wave_h, wave), (wo1_h, wo1), (wq2_h, wq2),
-             (wk2_h, wk2), (wv2_h, wv2), (wo2_h, wo2), (wg_h, wg), (wu_h, wu), (wd_h, wd)]
-        )
-    ]
-    for load in loads:
-        load.start()
-
     barrier = pltpu.get_barrier_semaphore()
 
     def greet(step, carry):
@@ -203,6 +194,20 @@
 
     lax.fori_loop(1, total, greet, 0)
 
+    loads = [
+        pltpu.make_async_copy(src, dst, local_sem.at[i])
+        for i, (src, dst) in enumerate(
+            [(fields_h, fields), (gain_lon_h, gain_lon), (wq1_h, wq1), (wk1_h, wk1), (wv1_h, wv1), (wave_h, wave), (wo1_h, wo1), (wq2_h, wq2),
+             (wk2_h, wk2), (wv2_h, wv2), (wo2_h, wo2), (wg_h, wg), (wu_h, wu), (wd_h, wd),
+             (gain_lat_h, gain_lat), (gain_mlp_h, gain_mlp), (temp_lon_h, temp_lon), (bias_lon_h, bias_lon),
+             (temp_lat_h, temp_lat), (bias_lat_h, bias_lat)]
+        )
+    ]
+    for load in loads:
+        load.start()
+
+    for load in loads[:2]:
+        load.wait()
     wide = fields[...].astype(F32)
     norm_out[...] = normalize(wide, gain_lon[...][None])
     pieces = wide.reshape(rows, n_lat, cols, depth).astype(BF16)
@@ -245,7 +250,8 @@
     spread = jnp.abs(lax.rem(hs, count) - lax.rem(hl, count)).astype(F32) / count
     mask = jnp.where(hs // count == hl // count, 0.0, -1e30).astype(F32)
 
-    for load in loads[:4]:
+    early = loads[2:6] + loads[16:18]
+    for load in early:
         load.wait()
     wq_t = wq1[...].T
     wv_t = wv1[...].T
@@ -258,36 +264,45 @@
     keys = mm(normed, wk1[...]).astype(BF16)
     queries_t = mm_nt(wq_t, normed).astype(BF16)
     values_t = mm_nt(wv_t, normed).astype(BF16)
-    att_t = heads_t(keys, queries_t, values_t, temp_lon, bias_lon, wave[...], None, heads, size)
-    att = mm_nt(eye, att_t)
-    att_out[...] = att.reshape(total, cols, depth).astype(BF16)
-
     my_row = me_lat * rows + me_lon
 
-    def att_copy(step):
-        peer = lax.rem(me + step, total)
+    def att_copy(peer, row):
         return pltpu.make_async_remote_copy(
-            src_ref=att_out.at[peer], dst_ref=att_in.at[my_row], send_sem=s3.at[step],
-            recv_sem=r3.at[step], device_id=(peer // n_lat, lax.rem(peer, n_lat)),
+            src_ref=att_out.at[peer], dst_ref=att_in.at[row], send_sem=s3.at[peer],
+            recv_sem=r3.at[row], device_id=(peer // n_lat, lax.rem(peer, n_lat)),
             device_id_type=MESH,
         )
 
-    def start_att(step, carry):
-        att_copy(step).start()
+    batch = min(nlon, 128)
+    group = batch // cols
+    for start in range(0, nlon, batch):
+        span = slice(start, start + batch)
+        att_t = heads_t(keys, queries_t[:, span], values_t, temp_lon, bias_lon, wave[:, span], None, heads, size)
+        att = mm_nt(eye[:batch, :batch], att_t)
+        first_peer = start // cols
+        att_out[first_peer:first_peer + group] = att.reshape(group, cols, depth).astype(BF16)
+
+        def start_att(step, carry, first_peer=first_peer):
+            peer = first_peer + lax.rem(me + step, group)
+
+            @pl.when(peer != me)
+            def _():
+                att_copy(peer, my_row).start()
+
+            return carry
+
+        lax.fori_loop(0, group, start_att, 0)
+    att_in[pl.ds(my_row, 1)] = att_out[pl.ds(me, 1)]
+
+    def wait_att(step, carry):
+        att_copy(lax.rem(me + step, total), lax.rem(my_row + step, count)).wait_recv()
         return carry
 
-    def wait_att(step, carry):
-        att_copy(step).wait_recv()
+    def wait_att_send(step, carry):
+        att_copy(lax.rem(me + step, total), my_row).wait_send()
         return carry
 
-    def wait_att_send(step, carry):
-        att_copy(step).wait_send()
-        return carry
-
-    lax.fori_loop(1, total, start_att, 0)
-    att_in[pl.ds(my_row, 1)] = att_out[pl.ds(me, 1)]
-
-    for load in loads[4:]:
+    for load in loads[6:16] + loads[18:]:
         load.wait()
     wq2_t = wq2[...].T
     wv2_t = wv2[...].T
@@ -321,15 +336,26 @@
         second = second + mm(hidden, wd[f:f + step_ff, :])
     upd_out[...] = second.reshape(n_lat, rows, cols, depth).astype(BF16)
 
-    sends4 = [lat_copy(step, upd_out, out, s4, r4) for step in range(1, n_lat)]
+    def upd_copy(step):
+        peer = lax.rem(me_lat + step, n_lat)
+        return pltpu.make_async_remote_copy(
+            src_ref=upd_out.at[peer], dst_ref=out.at[:, pl.ds(pl.multiple_of(me_lat * cols, cols), cols), :],
+            send_sem=s4.at[step], recv_sem=r4.at[step], device_id=(me_lon, peer), device_id_type=MESH,
+        )
+
+    sends4 = [upd_copy(step) for step in range(1, n_lat)]
     for copy in sends4:
         copy.start()
-    out[pl.ds(me_lat, 1)] = upd_out[pl.ds(me_lat, 1)]
+    own = pltpu.make_async_copy(
+        upd_out.at[me_lat], out.at[:, pl.ds(pl.multiple_of(me_lat * cols, cols), cols), :], s4.at[0]
+    )
+    own.start()
     for copy in sends1:
         copy.wait_send()
     for copy in sends2:
         copy.wait_send()
     lax.fori_loop(1, total, wait_att_send, 0)
+    own.wait()
     for copy in sends4:
         copy.wait()
 
@@ -347,18 +373,19 @@
     total = n_lon * n_lat
     place = np.arange(nlon)
     wave = np.cos((place[:, None] - place[None, :]) * (2.0 * math.pi / nlon)).astype(np.float32)
-    vmem = pl.BlockSpec(memory_space=pltpu.VMEM)
-    smem = pl.BlockSpec(memory_space=pltpu.SMEM)
     hbm = pl.BlockSpec(memory_space=pl.ANY)
     weights = (query_lon, key_lon, value_lon, out_lon, query_lat, key_lat, value_lat, out_lat,
                w_gate, w_up, w_down)
     dma = pltpu.SemaphoreType.DMA
     updated = pl.pallas_call(
         functools.partial(block_kernel, n_lon, n_lat, rows, width, depth, heads),
-        out_shape=jax.ShapeDtypeStruct((n_lat, rows, cols, depth), BF16),
-        in_specs=[vmem] * 4 + [smem] * 4 + [hbm] * 12,
-        out_specs=vmem,
-        scratch_shapes=[pltpu.VMEM((nlon, nlon), F32)]
+        out_shape=jax.ShapeDtypeStruct((rows, width, depth), BF16),
+        in_specs=[hbm] * 20,
+        out_specs=hbm,
+        scratch_shapes=[pltpu.VMEM((rows, width, depth), BF16)]
+        + [pltpu.VMEM((1, depth), F32)] * 3
+        + [pltpu.VMEM((1, heads), F32)] * 4
+        + [pltpu.VMEM((nlon, nlon), F32)]
         + [pltpu.VMEM(w.shape, w.dtype) for w in weights]
         + [
             pltpu.VMEM((rows, width, depth), BF16),
@@ -368,7 +395,7 @@
             pltpu.VMEM((total, cols, depth), BF16),
             pltpu.VMEM((n_lat * rows, cols, depth), BF16),
             pltpu.VMEM((n_lat, rows, cols, depth), BF16),
-            dma((12,)),
+            dma((20,)),
             dma((n_lon,)), dma((n_lon,)),
             dma((n_lat,)), dma((n_lat,)),
             dma((total,)), dma((total,)),
@@ -376,10 +403,11 @@
         ],
         compiler_params=pltpu.CompilerParams(collective_id=0, has_side_effects=True),
     )(
-        fields, norm_lon[None], norm_lat[None], norm_mlp[None], temp_lon, bias_lon, temp_lat, bias_lat,
+        fields, norm_lon[None], norm_lat[None], norm_mlp[None], temp_lon[None], bias_lon[None],
+        temp_lat[None], bias_lat[None],
         jnp.asarray(wave), *weights,
     )
-    return jnp.transpose(updated, (1, 0, 2, 3)).reshape(rows, width, depth)
+    return updated
 
 
 def choose(*args):

time: 31.8 us -> 27.3 us (0.86); the launches traced: 31.7 us -> 26.8 us
  Pallas kernels: 30.1 us -> 25.2 us
    pallas_call x1, Pallas kernels: 30.1 us -> 25.2 us  [fused_body(): pl.pallas_call(functools.partial(block_kernel, n_lon, n_lat, rows, width,...]
    reshape x1 -> x0, local copies, waits for them, and re-layouts: 1.57 us -> none  [fused_body(): return jnp.transpose(updated, (1, 0, 2, 3)).reshape(rows, width, depth)]
    unnamed x0 -> x1, local copies, waits for them, and re-layouts: none -> 1.57 us
where the time goes in v2:
time: 27.3 us; the launch traced here: 26.8 us
  Pallas kernels  25.2 us (92%)
  local copies, waits for them, and re-layouts  1.57 us (6%)
    pallas_call x1, Pallas kernels, fused_body(): pl.pallas_call(functools.partial(block_kernel, n_lon, n_lat, rows, width,...  25.2 us
    unnamed x1, local copies, waits for them, and re-layouts  1.57 us

profile of v2, /device:TPU:0, one launch (start us, length us, event | category | flops | bytes accessed | tf_op | source)
XLA Modules:
  0.0 26.8 jit_solution(6616730889454116283)
XLA Ops:
  0.0 25.2 %shard_map.190 = bf16[8,32,256]{2,1,0:T(8,128)(2,1)} custom-call(bf16[8,32,256]{2,1,0:T(8,128)(2,1)} %fields_h.1, f32[1,256]{1,0:T(1,128)} %bitcast.7, f32[1,256]{1,0:T(1,128)} %bitcast.8, f32[1,256]{1,0:T(1,128)} %bitcast.9, f32[1,8]{1,0:T(1,128)} %bitcast.10, f32[1,8]{1,0:T(1,128)} %bitcast.11, f32[1,8]{1,0:T(1,128)} %bitcast.12, f32[1,8]{1,0:T(1,128)} %bitcast.13, ...), custom_call_target="tpu_custom_call" | custom-call | tf_op jit(solution)/shard_map/pallas_call | solution.py:380
  25.2 1.6 %copy.22 = bf16[8,32,256]{2,1,0:T(8,128)(2,1)} copy(bf16[8,32,256]{2,1,0:T(8,128)(2,1)} %shard_map.190) | data formatting | bytes 262144

commit v3 on v2

--- a/solution.py
+++ b/solution.py
@@ -379,7 +379,7 @@
     dma = pltpu.SemaphoreType.DMA
     updated = pl.pallas_call(
         functools.partial(block_kernel, n_lon, n_lat, rows, width, depth, heads),
-        out_shape=jax.ShapeDtypeStruct((rows, width, depth), BF16),
+        out_shape=pltpu.VMEM((rows, width, depth), BF16),
         in_specs=[hbm] * 20,
         out_specs=hbm,
         scratch_shapes=[pltpu.VMEM((rows, width, depth), BF16)]

time: 27.3 us -> 26.3 us (0.963)
  local copies, waits for them, and re-layouts: 1.57 us -> 0.66 us
    unnamed x1, local copies, waits for them, and re-layouts: 1.57 us -> 0.66 us
where the time goes in v3:
time: 26.3 us; the launch traced here: 25.8 us
  Pallas kernels  25.1 us (95%)
  local copies, waits for them, and re-layouts  0.66 us (3%)
    pallas_call x1, Pallas kernels, fused_body(): pl.pallas_call(functools.partial(block_kernel, n_lon, n_lat, rows, width,...  25.1 us
    unnamed x1, local copies, waits for them, and re-layouts  0.66 us

profile of v3, /device:TPU:0, one launch (start us, length us, event | category | flops | bytes accessed | tf_op | source)
XLA Modules:
  0.0 25.8 jit_solution(8919091077955762233)
XLA Ops:
  0.0 25.1 %shard_map.190 = bf16[8,32,256]{2,1,0:T(8,128)(2,1)S(1)} custom-call(bf16[8,32,256]{2,1,0:T(8,128)(2,1)} %fields_h.1, f32[1,256]{1,0:T(1,128)} %bitcast.7, f32[1,256]{1,0:T(1,128)} %bitcast.8, f32[1,256]{1,0:T(1,128)} %bitcast.9, f32[1,8]{1,0:T(1,128)} %bitcast.10, f32[1,8]{1,0:T(1,128)} %bitcast.11, f32[1,8]{1,0:T(1,128)} %bitcast.12, f32[1,8]{1,0:T(1,128)} %bitcast.13, ...), custom_call_target="tpu_custom_call" | custom-call | tf_op jit(solution)/shard_map/pallas_call | solution.py:380
  25.1 0.7 %copy.22 = bf16[8,32,256]{2,1,0:T(8,128)(2,1)} copy(bf16[8,32,256]{2,1,0:T(8,128)(2,1)S(1)} %shard_map.190) | data formatting | bytes 262144

commit v4 on v3

--- a/solution.py
+++ b/solution.py
@@ -171,7 +171,7 @@
     out,
     fields, gain_lon, gain_lat, gain_mlp, temp_lon, bias_lon, temp_lat, bias_lat,
     wave, wq1, wk1, wv1, wo1, wq2, wk2, wv2, wo2, wg, wu, wd,
-    norm_out, norm_in, field_out, field_in, att_out, att_in, upd_out,
+    norm_out, norm_in, field_out, field_in, att_out, att_in, upd_out, query_s, first_s, mixed_s,
     local_sem, s1, r1, s2, r2, s3, r3, s4, r4,
 ):
     me_lon = lax.axis_index("lon")
@@ -262,7 +262,7 @@
     nlon = n_lon * width
     normed = norm_in[...].reshape(nlon, depth)
     keys = mm(normed, wk1[...]).astype(BF16)
-    queries_t = mm_nt(wq_t, normed).astype(BF16)
+    query_s[...] = mm_nt(wq_t, normed).astype(BF16)
     values_t = mm_nt(wv_t, normed).astype(BF16)
     my_row = me_lat * rows + me_lon
 
@@ -275,15 +275,19 @@
 
     batch = min(nlon, 128)
     group = batch // cols
-    for start in range(0, nlon, batch):
-        span = slice(start, start + batch)
-        att_t = heads_t(keys, queries_t[:, span], values_t, temp_lon, bias_lon, wave[:, span], None, heads, size)
+    lons = group // n_lat
+    high = (2 * me_lat) // n_lat
+    for turn in range(1, total // group + 1):
+        part = lax.rem(me // group + turn, total // group)
+        span = pl.ds(pl.multiple_of(part * batch, batch), batch)
+        att_t = heads_t(keys, query_s[:, span], values_t, temp_lon, bias_lon, wave[:, span], None, heads, size)
         att = mm_nt(eye[:batch, :batch], att_t)
-        first_peer = start // cols
-        att_out[first_peer:first_peer + group] = att.reshape(group, cols, depth).astype(BF16)
-
-        def start_att(step, carry, first_peer=first_peer):
-            peer = first_peer + lax.rem(me + step, group)
+        att_out[pl.ds(part * group, group)] = att.reshape(group, cols, depth).astype(BF16)
+
+        def start_att(step, carry, part=part):
+            away = step // lons
+            lat_peer = away + (1 - high) * (n_lat - 1 - 2 * away)
+            peer = (part * lons + lax.rem(me_lon + step, lons)) * n_lat + lat_peer
 
             @pl.when(peer != me)
             def _():
@@ -324,30 +328,38 @@
                     spread, mask, heads, size)
         )
     att_t = jnp.concatenate(parts, axis=1)
-    attended = mm_nt(from_cols, att_t).astype(BF16)
-    second = first + mm(attended, wo2[...])
-    normed = normalize(second, gain_mlp[...])
+    mixed_s[...] = mm_nt(from_cols, att_t).astype(BF16)
+    first_s[...] = first
+
+    def upd_copy(peer, owner):
+        return pltpu.make_async_remote_copy(
+            src_ref=upd_out.at[peer], dst_ref=out.at[:, pl.ds(pl.multiple_of(me_lat * cols, cols), cols), :],
+            send_sem=s4.at[peer], recv_sem=r4.at[owner], device_id=(me_lon, peer), device_id_type=MESH,
+        )
+
     ff = wg.shape[1]
     step_ff = min(ff, 256)
-    for f in range(0, ff, step_ff):
-        gate = mm(normed, wg[:, f:f + step_ff])
-        upper = mm(normed, wu[:, f:f + step_ff])
-        hidden = (gate / (1.0 + jnp.exp(-gate)) * upper).astype(BF16)
-        second = second + mm(hidden, wd[f:f + step_ff, :])
-    upd_out[...] = second.reshape(n_lat, rows, cols, depth).astype(BF16)
-
-    def upd_copy(step):
-        peer = lax.rem(me_lat + step, n_lat)
-        return pltpu.make_async_remote_copy(
-            src_ref=upd_out.at[peer], dst_ref=out.at[:, pl.ds(pl.multiple_of(me_lat * cols, cols), cols), :],
-            send_sem=s4.at[step], recv_sem=r4.at[step], device_id=(me_lon, peer), device_id_type=MESH,
-        )
-
-    sends4 = [upd_copy(step) for step in range(1, n_lat)]
-    for copy in sends4:
-        copy.start()
+    near = n_lat // 2
+    for turn in range(1, 3):
+        part = lax.rem(high + turn, 2)
+        span = pl.ds(pl.multiple_of(part * half, half), half)
+        second = first_s[span, :] + mm(mixed_s[span, :], wo2[...])
+        normed = normalize(second, gain_mlp[...])
+        for f in range(0, ff, step_ff):
+            gate = mm(normed, wg[:, f:f + step_ff])
+            upper = mm(normed, wu[:, f:f + step_ff])
+            hidden = (gate / (1.0 + jnp.exp(-gate)) * upper).astype(BF16)
+            second = second + mm(hidden, wd[f:f + step_ff, :])
+        upd_out[pl.ds(part * near, near)] = second.reshape(near, rows, cols, depth).astype(BF16)
+        for away in range(near):
+            peer = part * near + away + (1 - high) * (near - 1 - 2 * away)
+
+            @pl.when(peer != me_lat)
+            def _(peer=peer):
+                upd_copy(peer, me_lat).start()
+
     own = pltpu.make_async_copy(
-        upd_out.at[me_lat], out.at[:, pl.ds(pl.multiple_of(me_lat * cols, cols), cols), :], s4.at[0]
+        upd_out.at[me_lat], out.at[:, pl.ds(pl.multiple_of(me_lat * cols, cols), cols), :], s4.at[me_lat]
     )
     own.start()
     for copy in sends1:
@@ -356,8 +368,9 @@
         copy.wait_send()
     lax.fori_loop(1, total, wait_att_send, 0)
     own.wait()
-    for copy in sends4:
-        copy.wait()
+    for step in range(1, n_lat):
+        peer = lax.rem(me_lat + step, n_lat)
+        upd_copy(peer, peer).wait()
 
 
 def fused_body(
@@ -395,6 +408,9 @@
             pltpu.VMEM((total, cols, depth), BF16),
             pltpu.VMEM((n_lat * rows, cols, depth), BF16),
             pltpu.VMEM((n_lat, rows, cols, depth), BF16),
+            pltpu.VMEM((depth, nlon), BF16),
+            pltpu.VMEM((rows * width, depth), F32),
+            pltpu.VMEM((rows * width, depth), BF16),
             dma((20,)),
             dma((n_lon,)), dma((n_lon,)),
             dma((n_lat,)), dma((n_lat,)),
@@ -413,7 +429,8 @@
 def choose(*args):
     rows, width, _ = args[0].shape
     n_lon, n_lat = lax.axis_size("lon"), lax.axis_size("lat")
-    if rows == n_lon and width % n_lat == 0 and width // n_lat == 8:
+    fits = rows == n_lon and width == 8 * n_lat and n_lat % 2 == 0 and 16 % n_lat == 0
+    if fits and (width * n_lon) % 256 == 0:
         return fused_body(*args)
     return body(*args)
 

time: 26.3 us -> 27.7 us (1.053); the launches traced: 25.8 us -> 27.5 us
  Pallas kernels: 25.1 us -> 26.8 us
    pallas_call x1, Pallas kernels: 25.1 us -> 26.8 us  [fused_body(): pl.pallas_call(functools.partial(block_kernel, n_lon, n_lat, rows, width,...]
where the time goes in v4:
time: 27.7 us; the launch traced here: 27.5 us
  Pallas kernels  26.8 us (97%)
  local copies, waits for them, and re-layouts  0.66 us (2%)
    pallas_call x1, Pallas kernels, fused_body(): pl.pallas_call(functools.partial(block_kernel, n_lon, n_lat, rows, width,...  26.8 us
    unnamed x1, local copies, waits for them, and re-layouts  0.66 us

profile of v4, /device:TPU:0, one launch (start us, length us, event | category | flops | bytes accessed | tf_op | source)
XLA Modules:
  0.0 27.5 jit_solution(1169340654465526616)
XLA Ops:
  0.0 26.8 %shard_map.190 = bf16[8,32,256]{2,1,0:T(8,128)(2,1)S(1)} custom-call(bf16[8,32,256]{2,1,0:T(8,128)(2,1)} %fields_h.1, f32[1,256]{1,0:T(1,128)} %bitcast.7, f32[1,256]{1,0:T(1,128)} %bitcast.8, f32[1,256]{1,0:T(1,128)} %bitcast.9, f32[1,8]{1,0:T(1,128)} %bitcast.10, f32[1,8]{1,0:T(1,128)} %bitcast.11, f32[1,8]{1,0:T(1,128)} %bitcast.12, f32[1,8]{1,0:T(1,128)} %bitcast.13, ...), custom_call_target="tpu_custom_call" | custom-call | tf_op jit(solution)/shard_map/pallas_call | solution.py:393
  26.9 0.7 %copy.22 = bf16[8,32,256]{2,1,0:T(8,128)(2,1)} copy(bf16[8,32,256]{2,1,0:T(8,128)(2,1)S(1)} %shard_map.190) | data formatting | bytes 262144
